TPU v7x, 32 devices: a 4x4x1 block of a 4x4x8 slice. The times are simulated.
32 devices in a mesh: stage: 1 (over z), data: 32 (over y, x, core).
Axes of the slice: x: 4, y: 4, z: 1, core: 2. Of those that a mesh axis runs over, the one named last changes fastest.
The devices are a block of a 4x4x8 slice.
Arguments:
- w_master: float32 [192, 1024, 512], P('stage', 'data')
- momentum: float32 [192, 1024, 512], P('stage', 'data')
- grad: bfloat16 [192, 1024, 512], P('stage', 'data')
Outputs:
- output 1: bfloat16 [192, 1024, 512], P('stage')
- output 2: float32 [192, 1024, 512], P('stage', 'data')
All inputs are finite; a program needn't handle non-finite values.
Results may differ from a plain program's by a relative error of at most 0.00787722.
Values are sent between devices in bfloat16 or wider.
A program may use at most 768 MiB of HBM per device.

v0:
```python
import math
import jax
import jax.numpy as jnp
from jax import lax
from jax.sharding import PartitionSpec as P

NS_ITERS = 5
MOMENTUM = 0.95
LEARN_RATE = 0.02
WEIGHT_DECAY = 0.1
NORM_EPS = 1e-7
COEF_A = 3.4445
COEF_B = -4.7750
COEF_C = 2.0315


def newton_schulz(x_mat):
    wide = x_mat.shape[1] <= x_mat.shape[2]
    for iteration in range(NS_ITERS):
        if wide:
            gram_mat = jnp.einsum("kip,kjp->kij", x_mat, x_mat, preferred_element_type=jnp.float32)
        else:
            gram_mat = jnp.einsum("kpi,kpj->kij", x_mat, x_mat, preferred_element_type=jnp.float32)
        gram_mat = gram_mat.astype(jnp.bfloat16)
        square = jnp.einsum("kij,kjl->kil", gram_mat, gram_mat, preferred_element_type=jnp.float32)
        poly_mat = (COEF_B * gram_mat.astype(jnp.float32) + COEF_C * square).astype(jnp.bfloat16)
        if wide:
            prod_mat = jnp.einsum("kij,kjp->kip", poly_mat, x_mat, preferred_element_type=jnp.float32)
        else:
            prod_mat = jnp.einsum("kpj,kij->kpi", x_mat, poly_mat, preferred_element_type=jnp.float32)
        x_mat = (COEF_A * x_mat.astype(jnp.float32) + prod_mat).astype(jnp.bfloat16)
    return x_mat


def solution(mesh):
    group = mesh.shape["data"]
    row_spec = P("stage", "data", None)
    full_spec = P("stage", None, None)

    def local_step(w_rows, mom_rows, grad_rows):
        mat_count, rows_dev, col_count = mom_rows.shape
        own_count = mat_count // group
        rms_scale = 0.2 * math.sqrt(max(rows_dev * group, col_count))
        mom_new = MOMENTUM * mom_rows + grad_rows.astype(jnp.float32)
        sq_total = lax.psum(jnp.sum(mom_new * mom_new, axis=(1, 2)), "data")
        owned = lax.all_to_all(mom_new.astype(jnp.bfloat16), "data", 0, 1, tiled=True)
        my_index = lax.axis_index("data")
        sq_owned = lax.dynamic_slice_in_dim(sq_total, my_index * own_count, own_count)
        x_mat = (owned.astype(jnp.float32) / (jnp.sqrt(sq_owned)[:, None, None] + NORM_EPS)).astype(jnp.bfloat16)
        x_mat = newton_schulz(x_mat)
        ortho_rows = lax.all_to_all(x_mat, "data", 1, 0, tiled=True)
        w_new = w_rows - LEARN_RATE * (ortho_rows.astype(jnp.float32) * rms_scale + WEIGHT_DECAY * w_rows)
        params = lax.all_gather(w_new.astype(jnp.bfloat16), "data", axis=1, tiled=True)
        return params, mom_new

    return jax.shard_map(local_step, mesh=mesh, in_specs=(row_spec, row_spec, row_spec), out_specs=(full_spec, row_spec), check_vma=False)
```

profile of v0, /device:TPU:97, one launch (start us, length us, event | category | flops | bytes accessed | tf_op | source)
XLA Modules:
  0.0 1116.4 jit_solution(18238679732850417733)
XLA Ops:
  7.2 13.6 %multiply_reduce_fusion = (f32[192]{0:T(256)S(1)}, f32[192,32,512]{2,1,0:T(8,128)}) fusion(bf16[192,32,512]{2,1,0:T(8,128)(2,1)} %param.5, f32[192,32,512]{2,1,0:T(8,128)} %param.4), kind=kLoop, calls=%fused_computation.12 | loop fusion | flops 15728448 | bytes 31458048 | tf_op jit(solution)/shard_map/reduce_sum | solution.py:45
  20.8 8.3 convert_element_type.106
  29.1 9.1 all-to-all-start
  38.2 0.1 all-gather.2.cloned.1.call-start
  38.3 119.2 %psum.7 = f32[192]{0:T(256)S(1)} all-reduce(f32[192]{0:T(256)S(1)} %get-tuple-element.2), channel_id=1, replica_groups=mesh['stage'=1,'data'=32] {'data'}, use_global_device_ids=true, to_apply=%region_1.0 | all-reduce | flops 192 | bytes 1536 | tf_op jit(solution)/shard_map/psum | solution.py:45
  157.5 0.1 sqrt_add_fusion
  157.6 0.0 all-to-all-done
  157.6 9.4 copy.12
  167.0 6.4 fusion
  173.4 0.0 copy-start
  173.4 2.7 copy-done
  176.1 4.9 convolution_convert_fusion.4
  181.0 17.2 %add_convert_fusion.4 = bf16[6,1024,512]{2,1,0:T(8,128)(2,1)} fusion(bf16[6,1024,512]{2,1,0:T(8,128)(2,1)} %copy-done, bf16[6,512,512]{2,1,0:T(8,128)(2,1)} %convolution_convert_fusion.4), kind=kOutput, calls=%fused_computation.11 | convolution fusion | flops 4852285440 | bytes 15728640 | tf_op jit(solution)/shard_map/kpj,kij->kpi/dot_general | solution.py:30
  198.3 8.1 convolution_convert_fusion.3
  206.3 10.9 add_convert_fusion.3
  217.2 8.1 convolution_convert_fusion.2
  225.3 11.1 add_convert_fusion.2
  236.3 8.1 convolution_convert_fusion.1
  244.4 10.9 add_convert_fusion.1
  255.3 8.1 convolution_convert_fusion
  263.3 10.9 add_convert_fusion
  274.3 6.5 copy.18
  280.8 106.1 %all_to_all.8 = bf16[6,1024,512]{2,0,1:T(8,128)(2,1)} all-to-all(bf16[6,1024,512]{2,0,1:T(8,128)(2,1)S(1)} %copy.18), channel_id=1, replica_groups=mesh['stage'=1,'data'=32] {'data'}, dimensions={1} | all-to-all | bytes 12582912 | tf_op jit(solution)/shard_map/all_to_all | solution.py:51
  386.9 12.1 %convert_multiply_fusion = f32[6,1024,512]{2,0,1:T(8,128)} fusion(bf16[6,1024,512]{2,0,1:T(8,128)(2,1)} %all_to_all.8), kind=kLoop, calls=%fused_computation | loop fusion | flops 6291456 | bytes 18874368 | tf_op jit(solution)/shard_map/mul | solution.py:52
  399.0 21.9 %copy.19 = f32[32,6,32,512]{3,2,1,0:T(8,128)} copy(f32[32,6,32,512]{3,1,2,0:T(8,128)} %bitcast.44) | data formatting | bytes 25165824 | tf_op jit(solution)/shard_map/mul | solution.py:52
  420.9 12.4 %fusion.3 = bf16[192,32,512]{2,1,0:T(8,128)(2,1)} fusion(f32[192,32,512]{2,1,0:T(8,128)} %param.3, f32[32,6,32,512]{3,2,1,0:T(8,128)} %copy.19), kind=kLoop, calls=%fused_computation.6 | loop fusion | flops 15728640 | bytes 31457280 | tf_op jit(solution)/shard_map/convert_element_type | solution.py:53
  433.3 0.1 all-gather.2.cloned.1.call-update
  433.3 544.8 %all-gather.2.cloned.1.call-done = bf16[192,1024,512]{2,1,0:T(8,128)(2,1)} async-done(((bf16[192,32,512]{2,1,0:T(8,128)(2,1)}), bf16[192,1024,512]{2,1,0:T(8,128)(2,1)}) %all-gather.2.cloned.1.call-update) | async-done | bytes 201326608 | tf_op jit(solution)/shard_map/all_gather | solution.py:53
  978.2 131.1 %copy.26 = bf16[192,1024,512]{2,1,0:T(8,128)(2,1)} copy(bf16[192,1024,512]{2,1,0:T(8,128)(2,1)} %all-gather.2.cloned.1.call-done) | data formatting | bytes 402653184
Async XLA Ops:
  29.1 128.5 %all-to-all-start = ((bf16[192,32,512]{2,1,0:T(8,128)(2,1)}), bf16[192,32,512]{2,1,0:T(8,128)(2,1)}, u32[]{:S(2)}, u32[]{:S(2)}) async-start(bf16[192,32,512]{2,1,0:T(8,128)(2,1)} %convert_element_type.106), calls=%async_computation | async-start | bytes 12582912 | tf_op jit(solution)/shard_map/all_to_all | solution.py:46
  38.2 939.9 %all-gather.2.cloned.1.call-start = ((), (), s32[]{:S(2)}) async-start(), calls=%async_computation.2 | async-start | bytes 207618048 | tf_op jit(solution)/shard_map/all_gather | solution.py:53
  173.4 2.7 copy-start
Sparse Core Ops, SparseCore 0:
  433.5 544.6 all-gather.1
where the time goes:
time: 1120 us
  waiting for transfers between devices  545 us (49%)
  blocking collectives  225 us (20%)
  local copies, waits for them, and re-layouts  172 us (15%)
  matrix products  98.1 us (9%)
  other arithmetic  52.9 us (5%)
  between operations  14.4 us (1%)
    all_gather x1, waiting for transfers between devices, local_step(): lax.all_gather(w_new.astype(jnp.bfloat16), 'data', axis=1, tiled=True)  545 us
    unnamed x3, local copies, waits for them, and re-layouts  134 us
    psum x1, blocking collectives, local_step(): sq_total = lax.psum(jnp.sum(mom_new * mom_new, axis=(1, 2)), 'data')  119 us
    all_to_all x1, blocking collectives, local_step(): ortho_rows = lax.all_to_all(x_mat, 'data', 1, 0, tiled=True)  106 us
    dot_general x5, matrix products, newton_schulz(): jnp.einsum('kpj,kij->kpi', x_mat, poly_mat, preferred_element_type=jnp.fl...  60.9 us
    dot_general x5, matrix products, newton_schulz(): jnp.einsum('kpi,kpj->kij', x_mat, x_mat, preferred_element_type=jnp.float32)  37.2 us
  transfers between devices with their start and end apart: 2, of which 1 were waited for; matrix products, arithmetic and copies ran while one was open for 0% of the time, Pallas kernels for 0%

commit v1 on v0

v1 whole, which is shorter than its diff:
```python
import functools
import math
import jax
import jax.numpy as jnp
from jax import lax
from jax.experimental import pallas as pl
from jax.experimental.pallas import tpu as pltpu
from jax.sharding import PartitionSpec as P

NS_ITERS = 5
MOMENTUM = 0.95
LEARN_RATE = 0.02
WEIGHT_DECAY = 0.1
NORM_EPS = 1e-7
COEF_A = 3.4445
COEF_B = -4.7750
COEF_C = 2.0315


def momentum_kernel(*refs):
    mom_ref, grad_ref = refs[:2]
    new_ref, half_ref, sq_ref = refs[-3:]
    mom_new = MOMENTUM * mom_ref[...] + grad_ref[...].astype(jnp.float32)
    new_ref[...] = mom_new
    half_ref[...] = mom_new.astype(jnp.bfloat16)
    rows_sum = jnp.sum(mom_new * mom_new, axis=1)
    lanes = sq_ref.shape[-1]
    total = rows_sum[:, :lanes]
    for start in range(lanes, rows_sum.shape[1], lanes):
        total = total + rows_sum[:, start:start + lanes]
    sq_ref[:, 0] = total


def momentum_step(mom_rows, grad_rows, mom_new, group, first, count):
    mats, rows, cols = mom_rows.shape
    whole = pl.BlockSpec((group, rows, cols), lambda i: (first + i, 0, 0))
    in_specs, operands, aliases = [whole, whole], [mom_rows, grad_rows], {}
    if mom_new is not None:
        in_specs.append(pl.BlockSpec(memory_space=pl.ANY))
        operands.append(mom_new)
        aliases = {2: 0}
    return pl.pallas_call(
        momentum_kernel,
        grid=(count,),
        out_shape=(
            jax.ShapeDtypeStruct(mom_rows.shape, jnp.float32),
            jax.ShapeDtypeStruct((count * group, rows, cols), jnp.bfloat16),
            jax.ShapeDtypeStruct((count * group, 1, 128), jnp.float32),
        ),
        in_specs=in_specs,
        out_specs=(
            whole,
            pl.BlockSpec((group, rows, cols), lambda i: (i, 0, 0)),
            pl.BlockSpec((group, 1, 128), lambda i: (i, 0, 0)),
        ),
        input_output_aliases=aliases,
        cost_estimate=pl.CostEstimate(flops=10 * count * group * rows * cols, bytes_accessed=12 * count * group * rows * cols, transcendentals=0),
        name="momentum_step",
    )(*operands)


def ns_kernel(chunk, sq_ref, x_in_ref, x_out_ref):
    norm = jnp.sqrt(jnp.sum(sq_ref[:, chunk])) + NORM_EPS
    x_mat = (x_in_ref[...].astype(jnp.float32) / norm).astype(jnp.bfloat16)
    for iteration in range(NS_ITERS):
        gram_mat = lax.dot_general(x_mat, x_mat, (((0,), (0,)), ((), ())), preferred_element_type=jnp.float32)
        gram_mat = gram_mat.astype(jnp.bfloat16)
        square = jnp.dot(gram_mat, gram_mat, preferred_element_type=jnp.float32)
        poly_mat = (COEF_B * gram_mat.astype(jnp.float32) + COEF_C * square).astype(jnp.bfloat16)
        prod_mat = jnp.dot(x_mat, poly_mat, preferred_element_type=jnp.float32)
        x_mat = (COEF_A * x_mat.astype(jnp.float32) + prod_mat).astype(jnp.bfloat16)
    x_out_ref[...] = x_mat


def newton_schulz(owned, sq_all, chunk):
    return pl.pallas_call(
        functools.partial(ns_kernel, chunk),
        out_shape=jax.ShapeDtypeStruct(owned.shape, owned.dtype),
        in_specs=[pl.BlockSpec(memory_space=pltpu.VMEM)] * 2,
        out_specs=pl.BlockSpec(memory_space=pltpu.VMEM),
        cost_estimate=pl.CostEstimate(flops=7 * 10**9, bytes_accessed=4 * owned.size, transcendentals=0),
        name="newton_schulz",
    )(sq_all, owned)


def update_kernel(rms_scale, *refs):
    w_ref, ortho_ref, out_ref = refs[0], refs[1], refs[-1]
    w_rows = w_ref[...]
    ortho = ortho_ref[...].astype(jnp.float32) * rms_scale
    out_ref[...] = (w_rows - LEARN_RATE * (ortho + WEIGHT_DECAY * w_rows)).astype(jnp.bfloat16)


def weight_update(w_rows, ortho_rows, partial, chunk, slot, slots, rms_scale):
    mats, rows, cols = ortho_rows.shape
    half = mats // 2
    in_specs = [
        pl.BlockSpec((half, rows, cols), lambda i: (2 * chunk + i, 0, 0)),
        pl.BlockSpec((half, rows, cols), lambda i: (i, 0, 0)),
    ]
    operands, aliases = [w_rows, ortho_rows], {}
    if partial is not None:
        in_specs.append(pl.BlockSpec(memory_space=pl.ANY))
        operands.append(partial)
        aliases = {2: 0}
    return pl.pallas_call(
        functools.partial(update_kernel, rms_scale),
        grid=(2,),
        out_shape=jax.ShapeDtypeStruct((slots * mats, rows, cols), jnp.bfloat16),
        in_specs=in_specs,
        out_specs=pl.BlockSpec((half, rows, cols), lambda i: (2 * slot + i, 0, 0)),
        input_output_aliases=aliases,
        name="weight_update",
    )(*operands)


def place_kernel(*refs):
    gathered_ref, out_ref = refs[0], refs[-1]
    for dev in range(gathered_ref.shape[0]):
        out_ref[:, dev] = gathered_ref[dev]


def place(gathered, params, first_mat, shape, block):
    group, mats, rows, cols = gathered.shape
    steps = mats // block
    in_specs = [pl.BlockSpec((group, block, rows, cols), lambda i: (0, i, 0, 0))]
    operands = [gathered]
    aliases = {}
    if params is not None:
        in_specs.append(pl.BlockSpec(memory_space=pl.ANY))
        operands.append(params)
        aliases = {1: 0}
    return pl.pallas_call(
        place_kernel,
        grid=(steps,),
        out_shape=jax.ShapeDtypeStruct(shape, gathered.dtype),
        in_specs=in_specs,
        out_specs=pl.BlockSpec((block, group, rows, cols), lambda i: (first_mat // block + i, 0, 0, 0)),
        input_output_aliases=aliases,
        cost_estimate=pl.CostEstimate(flops=1 * 10**7, bytes_accessed=4 * gathered.size, transcendentals=0),
        name="place",
    )(*operands)


def after(value, *others):
    return lax.optimization_barrier((value, *others))[0] if others else value


def gather_plan(chunks):
    plan, first = [(0, 1)], 1
    while first < chunks:
        count = min(2, chunks - first)
        plan.append((first, count))
        first += count
    return plan


def solution(mesh):
    group = mesh.shape["data"]
    row_spec = P("stage", "data", None)
    full_spec = P("stage", None, None)

    def local_step(w_rows, mom_rows, grad_rows):
        mat_count, rows_dev, col_count = mom_rows.shape
        chunks = mat_count // group
        rms_scale = 0.2 * math.sqrt(max(rows_dev * group, col_count))
        mom_new, half_first, sq_first = momentum_step(mom_rows, grad_rows, None, group, 0, 1)
        sq_first = lax.all_to_all(sq_first, "data", 0, 0, tiled=True)
        shape = (mat_count, group, rows_dev, col_count)
        params, waiting, ahead = None, [], ()
        for first, count in gather_plan(chunks):
            w_new = None
            for chunk in range(first, first + count):
                if chunk == 0:
                    half, sq_all, sq_index = half_first, sq_first, 0
                else:
                    if chunk == 1:
                        mom_new = after(mom_new, *ahead)
                        mom_new, half_rest, sq_rest = momentum_step(mom_rows, grad_rows, mom_new, group, 1, chunks - 1)
                        sq_rest = sq_rest.reshape(chunks - 1, group, 128).transpose(1, 0, 2)
                        sq_rest = lax.all_to_all(sq_rest, "data", 0, 0, tiled=True)
                    half, sq_all, sq_index = half_rest[(chunk - 1) * group:chunk * group], sq_rest, chunk - 1
                half = after(half, *ahead)
                owned = lax.all_to_all(half, "data", 0, 0, tiled=True)
                x_mat = newton_schulz(owned.reshape(rows_dev * group, col_count), sq_all, sq_index)
                ortho_rows = lax.all_to_all(x_mat.reshape(group, rows_dev, col_count), "data", 0, 0, tiled=True)
                w_new = weight_update(w_rows, ortho_rows, w_new, chunk, chunk - first, count, rms_scale)
                ahead = (w_new,)
            waiting.append((lax.all_gather(w_new, "data", axis=0, tiled=False), first * group))
            if len(waiting) > 2:
                gathered, place_mat = waiting.pop(0)
                params = place(after(gathered, w_new), params, place_mat, shape, 2)
                ahead = (w_new, params)
        for gathered, place_mat in waiting:
            params = place(gathered, params, place_mat, shape, 2)
        return params.reshape(mat_count, group * rows_dev, col_count), mom_new

    return jax.shard_map(local_step, mesh=mesh, in_specs=(row_spec, row_spec, row_spec), out_specs=(full_spec, row_spec), check_vma=False)
```

time: 1120 us -> 855 us (0.76)
  waiting for transfers between devices: 545 us -> 210 us
  Pallas kernels: 0 us -> 258 us
  local copies, waits for them, and re-layouts: 172 us -> 6.04 us
  blocking collectives: 225 us -> 353 us
  matrix products: 98.1 us -> 0 us
  other arithmetic: 52.9 us -> 0 us
    all_gather x1 -> x4, waiting for transfers between devices: 545 us -> 206 us  [local_step(): lax.all_gather(w_new, 'data', axis=0, tiled=False)]
    pallas_call x0 -> x18, Pallas kernels: none -> 258 us  [the longest x4 163 us: place(): pl.pallas_call(place_kernel, grid=(steps,), out_shape=jax.ShapeDtypeStruc...]
    all_to_all x1 -> x13, blocking collectives: 106 us -> 353 us  [the longest x6 170 us: local_step(): owned = lax.all_to_all(half, 'data', 0, 0, tiled=True)]
    unnamed x3 -> x2, local copies, waits for them, and re-layouts: 134 us -> 0.01 us
    psum x1 -> x0, blocking collectives: 119 us -> none  [local_step(): sq_total = lax.psum(jnp.sum(mom_new * mom_new, axis=(1, 2)), 'data')]
    dot_general x10 -> x0, matrix products: 98.1 us -> none  [the longest x5 60.9 us: newton_schulz(): jnp.einsum('kpj,kij->kpi', x_mat, poly_mat, preferred_element_type=jnp.fl...]
    convert_element_type x3 -> x0, other arithmetic: 27.1 us -> none  [the longest x1 12.4 us: local_step(): w_new.astype(jnp.bfloat16)]
    mul x1 -> x0, local copies, waits for them, and re-layouts: 21.9 us -> none  [local_step(): ortho_rows.astype(jnp.float32) * rms_scale + WEIGHT_DECAY * w_rows]
  transfers between devices with their start and end apart: 2 -> 5, of which waited for: 1 -> 4; matrix products, arithmetic and copies ran while one was open for 0% -> 1% of each run, Pallas kernels for 0% -> 25%
where the time goes in v1:
time: 855 us; the launch traced here: 846 us
  blocking collectives  353 us (41%)
  Pallas kernels  258 us (30%)
  waiting for transfers between devices  210 us (25%)
  between operations  14.3 us (2%)
    all_gather x4, waiting for transfers between devices, local_step(): lax.all_gather(w_new, 'data', axis=0, tiled=False)  206 us
    all_to_all x6, blocking collectives, local_step(): owned = lax.all_to_all(half, 'data', 0, 0, tiled=True)  170 us
    all_to_all x6, blocking collectives, local_step(): lax.all_to_all(x_mat.reshape(group, rows_dev, col_count), 'data', 0, 0, t...  167 us
    pallas_call x4, Pallas kernels, place(): pl.pallas_call(place_kernel, grid=(steps,), out_shape=jax.ShapeDtypeStruc...  163 us
    pallas_call x6, Pallas kernels, newton_schulz(): pl.pallas_call(functools.partial(ns_kernel, chunk), out_shape=jax.ShapeDt...  61 us
    pallas_call x6, Pallas kernels, weight_update(): pl.pallas_call(functools.partial(update_kernel, rms_scale), grid=(2,), ou...  17.2 us
  transfers between devices with their start and end apart: 5, of which 4 were waited for; matrix products, arithmetic and copies ran while one was open for 1% of the time, Pallas kernels for 25%

profile of v1, /device:TPU:97, one launch (start us, length us, event | category | flops | bytes accessed | tf_op | source)
XLA Modules:
  0.0 845.9 jit_solution(3119375660464013256)
XLA Ops:
  7.2 0.1 all-gather.9.cloned.1.call-start
  7.2 3.9 momentum_step.2
  11.1 15.9 %all_to_all.70.sq_ref = f32[32,1,128]{2,1,0:T(1,128)} all-to-all(f32[32,1,128]{2,1,0:T(1,128)} %get-tuple-element.17), channel_id=1, replica_groups=mesh['stage'=1,'data'=32] {'data'}, dimensions={0} | all-to-all | bytes 32768 | tf_op jit(solution)/shard_map/all_to_all | solution.py:167
  27.0 20.4 %all_to_all.71 = bf16[32,32,512]{2,1,0:T(8,128)(2,1)} all-to-all(bf16[32,32,512]{2,1,0:T(8,128)(2,1)} %get-tuple-element.18), channel_id=1, replica_groups=mesh['stage'=1,'data'=32] {'data'}, dimensions={0} | all-to-all | bytes 2097152 | tf_op jit(solution)/shard_map/all_to_all | solution.py:183
  47.3 10.1 %newton_schulz.6 = bf16[1024,512]{1,0:T(8,128)(2,1)} custom-call(f32[32,1,128]{2,1,0:T(1,128)} %all_to_all.70.sq_ref, bf16[1024,512]{1,0:T(8,128)(2,1)} %bitcast.23), custom_call_target="tpu_custom_call" | custom-call | flops 7000000000 | bytes 2097152 | tf_op jit(solution)/shard_map/newton_schulz/pallas_call | solution.py:76
  57.5 21.3 %all_to_all.72.refs_1_ = bf16[32,32,512]{2,1,0:T(8,128)(2,1)} all-to-all(bf16[32,32,512]{2,1,0:T(8,128)(2,1)} %bitcast.24), channel_id=1, replica_groups=mesh['stage'=1,'data'=32] {'data'}, dimensions={0} | all-to-all | bytes 2097152 | tf_op jit(solution)/shard_map/all_to_all | solution.py:185
  78.8 2.9 weight_update.6
  81.6 0.1 all-gather.9.cloned.1.call-update
  81.7 13.1 %momentum_step.3 = (f32[192,32,512]{2,1,0:T(8,128)}, bf16[160,32,512]{2,1,0:T(8,128)(2,1)}, f32[160,1,128]{2,1,0:T(1,128)}) custom-call(f32[192,32,512]{2,1,0:T(8,128)} %refs_0_.10, bf16[192,32,512]{2,1,0:T(8,128)(2,1)} %refs_1_.3, f32[192,32,512]{2,1,0:T(8,128)} %get-tuple-element.19.refs_2_), custom_call_target="tpu_custom_call", output_to_operand_aliasing={{0}: (2, {})} | custom-call | flops 26214400 | bytes 31457280 | tf_op jit(solution)/shard_map/momentum_step/pallas_call | solution.py:42
  94.8 1.6 copy.14
  96.4 4.3 all-to-all-start.3
  100.7 0.1 all-gather.15.cloned.1.call-start
  100.8 4.5 fusion
  105.2 4.2 all-to-all-done.3.sq_ref
  109.4 0.0 copy-start
  109.4 28.0 %all_to_all.73 = bf16[32,32,512]{2,1,0:T(8,128)(2,1)} all-to-all(bf16[32,32,512]{2,1,0:T(8,128)(2,1)} %get-tuple-element.22), channel_id=1, replica_groups=mesh['stage'=1,'data'=32] {'data'}, dimensions={0} | all-to-all | bytes 2097152 | tf_op jit(solution)/shard_map/all_to_all | solution.py:183
  137.4 0.0 copy-done
  137.4 10.2 %newton_schulz.7 = bf16[1024,512]{1,0:T(8,128)(2,1)} custom-call(f32[32,5,128]{2,1,0:T(8,128)} %copy-done, bf16[1024,512]{1,0:T(8,128)(2,1)} %bitcast.27), custom_call_target="tpu_custom_call" | custom-call | flops 7000000000 | bytes 2097152 | tf_op jit(solution)/shard_map/newton_schulz/pallas_call | solution.py:76
  147.6 30.4 %all_to_all.74.refs_1_ = bf16[32,32,512]{2,1,0:T(8,128)(2,1)} all-to-all(bf16[32,32,512]{2,1,0:T(8,128)(2,1)} %bitcast.28), channel_id=1, replica_groups=mesh['stage'=1,'data'=32] {'data'}, dimensions={0} | all-to-all | bytes 2097152 | tf_op jit(solution)/shard_map/all_to_all | solution.py:185
  178.0 2.9 weight_update.7.refs_2_
  180.9 32.2 %all_to_all.75 = bf16[32,32,512]{2,1,0:T(8,128)(2,1)} all-to-all(bf16[32,32,512]{2,1,0:T(8,128)(2,1)} %get-tuple-element.23), channel_id=1, replica_groups=mesh['stage'=1,'data'=32] {'data'}, dimensions={0} | all-to-all | bytes 2097152 | tf_op jit(solution)/shard_map/all_to_all | solution.py:183
  213.1 10.2 %newton_schulz.8 = bf16[1024,512]{1,0:T(8,128)(2,1)} custom-call(f32[32,5,128]{2,1,0:T(8,128)} %copy-done, bf16[1024,512]{1,0:T(8,128)(2,1)} %bitcast.29), custom_call_target="tpu_custom_call" | custom-call | flops 7000000000 | bytes 2097152 | tf_op jit(solution)/shard_map/newton_schulz/pallas_call | solution.py:76
  223.3 22.7 %all_to_all.76.refs_1_ = bf16[32,32,512]{2,1,0:T(8,128)(2,1)} all-to-all(bf16[32,32,512]{2,1,0:T(8,128)(2,1)} %bitcast.30), channel_id=1, replica_groups=mesh['stage'=1,'data'=32] {'data'}, dimensions={0} | all-to-all | bytes 2097152 | tf_op jit(solution)/shard_map/all_to_all | solution.py:185
  246.0 2.8 weight_update.8
  248.8 0.1 all-gather.15.cloned.1.call-update
  248.9 0.1 all-gather.13.cloned.1.call-start
  249.0 27.5 %all_to_all.77 = bf16[32,32,512]{2,1,0:T(8,128)(2,1)} all-to-all(bf16[32,32,512]{2,1,0:T(8,128)(2,1)S(1)} %get-tuple-element.24), channel_id=1, replica_groups=mesh['stage'=1,'data'=32] {'data'}, dimensions={0} | all-to-all | bytes 2097152 | tf_op jit(solution)/shard_map/all_to_all | solution.py:183
  276.4 10.2 %newton_schulz.9 = bf16[1024,512]{1,0:T(8,128)(2,1)} custom-call(f32[32,5,128]{2,1,0:T(8,128)} %copy-done, bf16[1024,512]{1,0:T(8,128)(2,1)} %bitcast.31), custom_call_target="tpu_custom_call" | custom-call | flops 7000000000 | bytes 2097152 | tf_op jit(solution)/shard_map/newton_schulz/pallas_call | solution.py:76
  286.6 27.4 %all_to_all.78.refs_1_ = bf16[32,32,512]{2,1,0:T(8,128)(2,1)} all-to-all(bf16[32,32,512]{2,1,0:T(8,128)(2,1)} %bitcast.32), channel_id=1, replica_groups=mesh['stage'=1,'data'=32] {'data'}, dimensions={0} | all-to-all | bytes 2097152 | tf_op jit(solution)/shard_map/all_to_all | solution.py:185
  314.0 2.9 weight_update.9.refs_2_
  316.9 30.7 %all_to_all.79 = bf16[32,32,512]{2,1,0:T(8,128)(2,1)} all-to-all(bf16[32,32,512]{2,1,0:T(8,128)(2,1)S(1)} %get-tuple-element.25), channel_id=1, replica_groups=mesh['stage'=1,'data'=32] {'data'}, dimensions={0} | all-to-all | bytes 2097152 | tf_op jit(solution)/shard_map/all_to_all | solution.py:183
  347.5 10.2 %newton_schulz.10 = bf16[1024,512]{1,0:T(8,128)(2,1)} custom-call(f32[32,5,128]{2,1,0:T(8,128)} %copy-done, bf16[1024,512]{1,0:T(8,128)(2,1)} %bitcast.33), custom_call_target="tpu_custom_call" | custom-call | flops 7000000000 | bytes 2097152 | tf_op jit(solution)/shard_map/newton_schulz/pallas_call | solution.py:76
  357.7 32.6 %all_to_all.80.refs_1_ = bf16[32,32,512]{2,1,0:T(8,128)(2,1)} all-to-all(bf16[32,32,512]{2,1,0:T(8,128)(2,1)} %bitcast.34), channel_id=1, replica_groups=mesh['stage'=1,'data'=32] {'data'}, dimensions={0} | all-to-all | bytes 2097152 | tf_op jit(solution)/shard_map/all_to_all | solution.py:185
  390.3 2.9 weight_update.10
  393.1 0.1 all-gather.13.cloned.1.call-update
  393.2 0.1 all-gather.11.cloned.1.call-start
  393.3 0.0 all-gather.9.cloned.1.call-done
  393.3 27.3 %place.4.refs_1_ = bf16[192,32,32,512]{3,2,1,0:T(8,128)(2,1)} custom-call(bf16[32,32,32,512]{3,2,1,0:T(8,128)(2,1)} %bitcast.21), custom_call_target="tpu_custom_call" | custom-call | flops 10000000 | bytes 67108864 | tf_op jit(solution)/shard_map/place/pallas_call | solution.py:132
  420.6 31.6 %all_to_all.81 = bf16[32,32,512]{2,1,0:T(8,128)(2,1)} all-to-all(bf16[32,32,512]{2,1,0:T(8,128)(2,1)S(1)} %get-tuple-element.27), channel_id=1, replica_groups=mesh['stage'=1,'data'=32] {'data'}, dimensions={0} | all-to-all | bytes 2097152 | tf_op jit(solution)/shard_map/all_to_all | solution.py:183
  452.2 10.2 %newton_schulz.11 = bf16[1024,512]{1,0:T(8,128)(2,1)} custom-call(f32[32,5,128]{2,1,0:T(8,128)} %copy-done, bf16[1024,512]{1,0:T(8,128)(2,1)} %bitcast.25), custom_call_target="tpu_custom_call" | custom-call | flops 7000000000 | bytes 2097152 | tf_op jit(solution)/shard_map/newton_schulz/pallas_call | solution.py:76
  462.4 32.3 %all_to_all.82.refs_1_ = bf16[32,32,512]{2,1,0:T(8,128)(2,1)} all-to-all(bf16[32,32,512]{2,1,0:T(8,128)(2,1)} %bitcast.26), channel_id=1, replica_groups=mesh['stage'=1,'data'=32] {'data'}, dimensions={0} | all-to-all | bytes 2097152 | tf_op jit(solution)/shard_map/all_to_all | solution.py:185
  494.7 2.9 weight_update.11
  497.6 0.1 all-gather.11.cloned.1.call-update
  497.7 7.4 all-gather.15.cloned.1.call-done
  505.0 54.1 %place.5.refs_1_ = bf16[192,32,32,512]{3,2,1,0:T(8,128)(2,1)} custom-call(bf16[32,64,32,512]{3,2,1,0:T(8,128)(2,1)} %bitcast.17.refs_0_, bf16[192,32,32,512]{3,2,1,0:T(8,128)(2,1)} %place.4.refs_1_), custom_call_target="tpu_custom_call", output_to_operand_aliasing={{}: (1, {})} | custom-call | flops 10000000 | bytes 134217728 | tf_op jit(solution)/shard_map/place/pallas_call | solution.py:132
  559.1 143.4 %all-gather.13.cloned.1.call-done = bf16[2048,32,512]{2,1,0:T(8,128)(2,1)} async-done(((bf16[64,32,512]{2,1,0:T(8,128)(2,1)}), bf16[2048,32,512]{2,1,0:T(8,128)(2,1)}) %all-gather.13.cloned.1.call-update) | async-done | bytes 67108880 | tf_op jit(solution)/shard_map/all_gather | solution.py:188
  702.5 54.1 %place.6.refs_1_ = bf16[192,32,32,512]{3,2,1,0:T(8,128)(2,1)} custom-call(bf16[32,64,32,512]{3,2,1,0:T(8,128)(2,1)} %bitcast.16.refs_0_, bf16[192,32,32,512]{3,2,1,0:T(8,128)(2,1)} %place.5.refs_1_), custom_call_target="tpu_custom_call", output_to_operand_aliasing={{}: (1, {})} | custom-call | flops 10000000 | bytes 134217728 | tf_op jit(solution)/shard_map/place/pallas_call | solution.py:132
  756.6 55.0 %all-gather.11.cloned.1.call-done = bf16[1024,32,512]{2,1,0:T(8,128)(2,1)} async-done(((bf16[32,32,512]{2,1,0:T(8,128)(2,1)}), bf16[1024,32,512]{2,1,0:T(8,128)(2,1)}) %all-gather.11.cloned.1.call-update) | async-done | bytes 33554448 | tf_op jit(solution)/shard_map/all_gather | solution.py:188
  811.7 27.3 %place.7 = bf16[192,32,32,512]{3,2,1,0:T(8,128)(2,1)} custom-call(bf16[32,32,32,512]{3,2,1,0:T(8,128)(2,1)} %bitcast.22, bf16[192,32,32,512]{3,2,1,0:T(8,128)(2,1)} %place.6.refs_1_), custom_call_target="tpu_custom_call", output_to_operand_aliasing={{}: (1, {})} | custom-call | flops 10000000 | bytes 67108864 | tf_op jit(solution)/shard_map/place/pallas_call | solution.py:132
Async XLA Ops:
  7.2 386.1 %all-gather.9.cloned.1.call-start = ((), (), s32[]{:S(2)}) async-start(), calls=%async_computation.14 | async-start | bytes 34603008 | tf_op jit(solution)/shard_map/all_gather | solution.py:188
  96.4 13.1 %all-to-all-start.3 = ((f32[32,5,128]{2,1,0:T(8,128)}), f32[32,5,128]{2,1,0:T(8,128)S(1)}, u32[]{:S(2)}, u32[]{:S(2)}) async-start(f32[32,5,128]{2,1,0:T(8,128)} %bitcast.20), calls=%async_computation.3 | async-start | bytes 262144 | tf_op jit(solution)/shard_map/all_to_all | solution.py:180
  100.7 404.3 %all-gather.15.cloned.1.call-start = ((), (), s32[]{:S(2)}) async-start(), calls=%async_computation.17 | async-start | bytes 69206016 | tf_op jit(solution)/shard_map/all_gather | solution.py:188
  109.4 28.0 %copy-start = (f32[32,5,128]{2,1,0:T(8,128)}, f32[32,5,128]{2,1,0:T(8,128)S(1)}, u32[]{:S(2)}) copy-start(f32[32,5,128]{2,1,0:T(8,128)S(1)} %all-to-all-done.3.sq_ref) | copy-start | bytes 245764
  248.9 453.6 %all-gather.13.cloned.1.call-start = ((), (), s32[]{:S(2)}) async-start(), calls=%async_computation.16 | async-start | bytes 69206016 | tf_op jit(solution)/shard_map/all_gather | solution.py:188
  393.2 418.5 %all-gather.11.cloned.1.call-start = ((), (), s32[]{:S(2)}) async-start(), calls=%async_computation.15 | async-start | bytes 34603008 | tf_op jit(solution)/shard_map/all_gather | solution.py:188
Sparse Core Ops, SparseCore 0:
  81.8 139.1 all-gather.8
  249.0 255.9 all-gather.14
  507.1 195.3 all-gather.12
  704.4 107.1 all-gather.10

commit v2 on v1

v2 whole, which is shorter than its diff:
```python
import functools
import math
import jax
import jax.numpy as jnp
from jax import lax
from jax.experimental import pallas as pl
from jax.experimental.pallas import tpu as pltpu
from jax.sharding import PartitionSpec as P

NS_ITERS = 5
MOMENTUM = 0.95
LEARN_RATE = 0.02
WEIGHT_DECAY = 0.1
NORM_EPS = 1e-7
COEF_A = 3.4445
COEF_B = -4.7750
COEF_C = 2.0315


def momentum_kernel(*refs):
    mom_ref, grad_ref = refs[:2]
    new_ref, half_ref, sq_ref = refs[-3:]
    mom_new = MOMENTUM * mom_ref[...] + grad_ref[...].astype(jnp.float32)
    new_ref[...] = mom_new
    half_ref[...] = mom_new.astype(jnp.bfloat16)
    rows_sum = jnp.sum(mom_new * mom_new, axis=1)
    lanes = sq_ref.shape[-1]
    total = rows_sum[:, :lanes]
    for start in range(lanes, rows_sum.shape[1], lanes):
        total = total + rows_sum[:, start:start + lanes]
    sq_ref[:, 0, 0] = total


def momentum_step(mom_rows, grad_rows, mom_new, group, first, count):
    mats, rows, cols = mom_rows.shape
    whole = pl.BlockSpec((group, rows, cols), lambda i: (first + i, 0, 0))
    in_specs, operands, aliases = [whole, whole], [mom_rows, grad_rows], {}
    if mom_new is not None:
        in_specs.append(pl.BlockSpec(memory_space=pl.ANY))
        operands.append(mom_new)
        aliases = {2: 0}
    return pl.pallas_call(
        momentum_kernel,
        grid=(count,),
        out_shape=(
            jax.ShapeDtypeStruct(mom_rows.shape, jnp.float32),
            jax.ShapeDtypeStruct((count * group, rows, cols), jnp.bfloat16),
            jax.ShapeDtypeStruct((group, count, 1, 128), jnp.float32),
        ),
        in_specs=in_specs,
        out_specs=(
            whole,
            pl.BlockSpec((group, rows, cols), lambda i: (i, 0, 0)),
            pl.BlockSpec((group, 1, 1, 128), lambda i: (0, i, 0, 0)),
        ),
        input_output_aliases=aliases,
        cost_estimate=pl.CostEstimate(flops=10 * count * group * rows * cols, bytes_accessed=12 * count * group * rows * cols, transcendentals=0),
        name="momentum_step",
    )(*operands)


def remote(src, dst, send_sem, recv_sem, device):
    return pltpu.make_async_remote_copy(
        src_ref=src, dst_ref=dst, send_sem=send_sem, recv_sem=recv_sem,
        device_id={"data": device}, device_id_type=pl.DeviceIdType.MESH)


def wait_bytes(ref, sem):
    pltpu.make_async_copy(ref, ref, sem).wait()


def send_blocks(group, source, landing, sems, lead):
    me = lax.axis_index("data")

    def send(step, carry):
        target = lax.rem(me + step, group)
        remote(source(target), landing.at[(*lead, me)], sems.at[(*lead, 0)], sems.at[(*lead, 1)], target).start()
        return carry

    lax.fori_loop(1, group, send, 0)


def exchange_kernel(group, first_mat, count, rms_scale, half_ref, sq_ref, w_ref, *refs):
    outs = refs[:-11]
    owned, ortho, x_buf, sq_buf, w_buf, in_sems, back_sems, sq_sems, own_sems, sq_own_sem, w_sem = refs[-11:]
    me = lax.axis_index("data")
    others = pl.ds(0, group - 1)
    rows, cols = owned.shape[-2:]
    load_w = pltpu.make_async_copy(w_ref.at[pl.ds(first_mat, count * group)], w_buf, w_sem)
    load_w.start()
    own_sq = pltpu.make_async_copy(sq_ref.at[me], sq_buf.at[me], sq_own_sem)
    own_sq.start()
    barrier = pltpu.get_barrier_semaphore()

    def greet(step, carry):
        pl.semaphore_signal(barrier, inc=1, device_id={"data": lax.rem(me + step, group)}, device_id_type=pl.DeviceIdType.MESH)
        return carry

    lax.fori_loop(1, group, greet, 0)
    pl.semaphore_wait(barrier, group - 1)

    send_blocks(group, lambda i: sq_ref.at[i], sq_buf, sq_sems, ())

    def own_block(chunk):
        return pltpu.make_async_copy(half_ref.at[chunk * group + me], owned.at[chunk, me], own_sems.at[chunk])

    def send_in(chunk, carry):
        send_blocks(group, lambda i: half_ref.at[chunk * group + i], owned, in_sems, (chunk,))
        own_block(chunk).start()
        return carry

    lax.fori_loop(0, count, send_in, 0)
    own_sq.wait()
    wait_bytes(sq_buf.at[others], sq_sems.at[1])

    def orthogonalize(chunk, carry):
        own_block(chunk).wait()
        wait_bytes(owned.at[chunk, others], in_sems.at[chunk, 1])
        norm = jnp.sqrt(jnp.sum(sq_buf[:, chunk])) + NORM_EPS
        x_mat = (owned[chunk].reshape(group * rows, cols).astype(jnp.float32) / norm).astype(jnp.bfloat16)
        for iteration in range(NS_ITERS):
            gram_mat = lax.dot_general(x_mat, x_mat, (((0,), (0,)), ((), ())), preferred_element_type=jnp.float32)
            gram_mat = gram_mat.astype(jnp.bfloat16)
            square = jnp.dot(gram_mat, gram_mat, preferred_element_type=jnp.float32)
            poly_mat = (COEF_B * gram_mat.astype(jnp.float32) + COEF_C * square).astype(jnp.bfloat16)
            prod_mat = jnp.dot(x_mat, poly_mat, preferred_element_type=jnp.float32)
            x_mat = (COEF_A * x_mat.astype(jnp.float32) + prod_mat).astype(jnp.bfloat16)
        x_buf[chunk] = x_mat.reshape(group, rows, cols)
        ortho[chunk, me] = x_buf[chunk, me]
        send_blocks(group, lambda i: x_buf.at[chunk, i], ortho, back_sems, (chunk,))
        return carry

    lax.fori_loop(0, count, orthogonalize, 0)

    load_w.wait()
    starts = [0]
    for out in outs:
        starts.append(starts[-1] + out.shape[0])
    for chunk in range(count):
        wait_bytes(ortho.at[chunk, others], back_sems.at[chunk, 1])
        for out, low, high in zip(outs, starts[:-1], starts[1:]):
            low_mat, high_mat = max(low, chunk * group), min(high, (chunk + 1) * group)

            def update(mat, carry, chunk=chunk, out=out, low=low):
                w_rows = w_buf[mat]
                o_rows = ortho[chunk, mat - chunk * group].astype(jnp.float32) * rms_scale
                out[mat - low] = (w_rows - LEARN_RATE * (o_rows + WEIGHT_DECAY * w_rows)).astype(jnp.bfloat16)
                return carry

            if low_mat < high_mat:
                lax.fori_loop(low_mat, high_mat, update, 0)

    wait_bytes(sq_buf.at[others], sq_sems.at[0])
    for chunk in range(count):
        wait_bytes(owned.at[chunk, others], in_sems.at[chunk, 0])
        wait_bytes(ortho.at[chunk, others], back_sems.at[chunk, 0])


def exchange(group, half, sq_part, w_rows, first_mat, splits, rms_scale, collective_id):
    mats, rows, cols = half.shape
    count = mats // group
    block = pltpu.VMEM((count, group, rows, cols), jnp.bfloat16)
    return pl.pallas_call(
        functools.partial(exchange_kernel, group, first_mat, count, rms_scale),
        out_shape=[jax.ShapeDtypeStruct((split, rows, cols), jnp.bfloat16) for split in splits],
        in_specs=[pl.BlockSpec(memory_space=pl.ANY)] * 3,
        out_specs=[pl.BlockSpec(memory_space=pltpu.VMEM)] * len(splits),
        scratch_shapes=[
            block,
            block,
            block,
            pltpu.VMEM(sq_part.shape, jnp.float32),
            pltpu.VMEM((mats, rows, cols), jnp.float32),
            pltpu.SemaphoreType.DMA((count, 2)),
            pltpu.SemaphoreType.DMA((count, 2)),
            pltpu.SemaphoreType.DMA((2,)),
            pltpu.SemaphoreType.DMA((count,)),
            pltpu.SemaphoreType.DMA,
            pltpu.SemaphoreType.DMA,
        ],
        compiler_params=pltpu.CompilerParams(collective_id=collective_id, has_side_effects=True, vmem_limit_bytes=56 * 2**20),
        cost_estimate=pl.CostEstimate(flops=count * 7 * 10**9, bytes_accessed=16 * half.size, transcendentals=0),
        name=f"exchange_{collective_id}",
    )(half, sq_part, w_rows)


def place_kernel(*refs):
    gathered_ref, out_ref = refs[0], refs[-1]
    for dev in range(gathered_ref.shape[0]):
        out_ref[:, dev] = gathered_ref[dev]


def place(gathered, params, first_mat, shape, block):
    group, mats, rows, cols = gathered.shape
    steps = mats // block
    in_specs = [pl.BlockSpec((group, block, rows, cols), lambda i: (0, i, 0, 0))]
    operands = [gathered]
    aliases = {}
    if params is not None:
        in_specs.append(pl.BlockSpec(memory_space=pl.ANY))
        operands.append(params)
        aliases = {1: 0}
    return pl.pallas_call(
        place_kernel,
        grid=(steps,),
        out_shape=jax.ShapeDtypeStruct(shape, gathered.dtype),
        in_specs=in_specs,
        out_specs=pl.BlockSpec((block, group, rows, cols), lambda i: (first_mat // block + i, 0, 0, 0)),
        input_output_aliases=aliases,
        cost_estimate=pl.CostEstimate(flops=1 * 10**7, bytes_accessed=4 * gathered.size, transcendentals=0),
        name="place",
    )(*operands)


def after(value, *others):
    return lax.optimization_barrier((value, *others))[0] if others else value


def stage_plan(chunks, group):
    first = min(2, chunks - 1)
    rest, last = (chunks - first) * group, 5 * group // 8
    return [(0, first, [first * group]), (first, chunks - first, [rest - last, last])]


def solution(mesh):
    group = mesh.shape["data"]
    row_spec = P("stage", "data", None)
    full_spec = P("stage", None, None)

    def local_step(w_rows, mom_rows, grad_rows):
        mat_count, rows_dev, col_count = mom_rows.shape
        chunks = mat_count // group
        rms_scale = 0.2 * math.sqrt(max(rows_dev * group, col_count))
        shape = (mat_count, group, rows_dev, col_count)
        mom_new, gathers, ahead = None, [], ()
        for number, (first, count, splits) in enumerate(stage_plan(chunks, group)):
            if mom_new is not None:
                mom_new = after(mom_new, *ahead)
            mom_new, half, sq_part = momentum_step(mom_rows, grad_rows, mom_new, group, first, count)
            ahead = exchange(group, half, sq_part, w_rows, first * group, splits, rms_scale, number)
            first_mat = first * group
            for w_new in ahead:
                gathers.append((lax.all_gather(w_new, "data", axis=0, tiled=False), first_mat))
                first_mat += w_new.shape[0]
        params = None
        for gathered, first_mat in gathers:
            params = place(gathered, params, first_mat, shape, 4)
        return params.reshape(mat_count, group * rows_dev, col_count), mom_new

    return jax.shard_map(local_step, mesh=mesh, in_specs=(row_spec, row_spec, row_spec), out_specs=(full_spec, row_spec), check_vma=False)
```

time: 855 us -> 776 us (0.908)
  blocking collectives: 353 us -> 0 us
  waiting for transfers between devices: 210 us -> 405 us
  Pallas kernels: 258 us -> 356 us
    all_to_all x13 -> x0, blocking collectives: 353 us -> none  [the longest x6 170 us: local_step(): owned = lax.all_to_all(half, 'data', 0, 0, tiled=True)]
    all_gather x4 -> x3, waiting for transfers between devices: 206 us -> 404 us  [local_step(): lax.all_gather(w_new, 'data', axis=0, tiled=False)]
    pallas_call x12 -> x2, Pallas kernels: 78.2 us -> 205 us  [exchange(): pl.pallas_call(functools.partial(exchange_kernel, group, first_mat, count...]
    pallas_call x4 -> x3, Pallas kernels: 163 us -> 137 us  [place(): pl.pallas_call(place_kernel, grid=(steps,), out_shape=jax.ShapeDtypeStruc...]
  transfers between devices with their start and end apart: 5 -> 3, of which waited for: 4 -> 3; matrix products, arithmetic and copies ran while one was open for 1% -> 0% of each run, Pallas kernels for 25% -> 35%
where the time goes in v2:
time: 776 us; the launch traced here: 775 us
  waiting for transfers between devices  405 us (52%)
  Pallas kernels  356 us (46%)
  between operations  13.8 us (2%)
    all_gather x3, waiting for transfers between devices, local_step(): lax.all_gather(w_new, 'data', axis=0, tiled=False)  404 us
    pallas_call x2, Pallas kernels, exchange(): pl.pallas_call(functools.partial(exchange_kernel, group, first_mat, count...  205 us
    pallas_call x3, Pallas kernels, place(): pl.pallas_call(place_kernel, grid=(steps,), out_shape=jax.ShapeDtypeStruc...  137 us
  transfers between devices with their start and end apart: 3, of which 3 were waited for; matrix products, arithmetic and copies ran while one was open for 0% of the time, Pallas kernels for 35%

profile of v2, /device:TPU:97, one launch (start us, length us, event | category | flops | bytes accessed | tf_op | source)
XLA Modules:
  0.0 775.4 jit_solution(9674718565080439416)
XLA Ops:
  7.2 0.1 all-gather.11.cloned.1.call-start
  7.2 5.0 momentum_step.2
  12.2 65.8 %exchange_0.1 = bf16[64,32,512]{2,1,0:T(8,128)(2,1)} custom-call(bf16[64,32,512]{2,1,0:T(8,128)(2,1)} %get-tuple-element.12.half_ref, f32[32,2,1,128]{3,2,1,0:T(1,128)} %get-tuple-element.13.sq_ref, f32[192,32,512]{2,1,0:T(8,128)} %w_ref.3), custom_call_target="tpu_custom_call" | custom-call | flops 14000000000 | bytes 16777216 | tf_op jit(solution)/shard_map/exchange_0/pallas_call | solution.py:163
  78.1 0.1 all-gather.11.cloned.1.call-update
  78.1 0.2 all-gather.9.cloned.1.call-start
  78.4 9.6 %momentum_step.3 = (f32[192,32,512]{2,1,0:T(8,128)}, bf16[128,32,512]{2,1,0:T(8,128)(2,1)}, f32[32,4,1,128]{3,2,1,0:T(1,128)}) custom-call(f32[192,32,512]{2,1,0:T(8,128)} %refs_0_.3, bf16[192,32,512]{2,1,0:T(8,128)(2,1)} %refs_1_.3, f32[192,32,512]{2,1,0:T(8,128)} %get-tuple-element.14.refs_2_), custom_call_target="tpu_custom_call", output_to_operand_aliasing={{0}: (2, {})} | custom-call | flops 20971520 | bytes 25165824 | tf_op jit(solution)/shard_map/momentum_step/pallas_call | solution.py:42
  88.0 138.9 %exchange_1.1 = (bf16[108,32,512]{2,1,0:T(8,128)(2,1)}, bf16[20,32,512]{2,1,0:T(8,128)(2,1)}) custom-call(bf16[128,32,512]{2,1,0:T(8,128)(2,1)} %get-tuple-element.15.half_ref, f32[32,4,1,128]{3,2,1,0:T(1,128)} %get-tuple-element.16.sq_ref, f32[192,32,512]{2,1,0:T(8,128)} %w_ref.3), custom_call_target="tpu_custom_call" | custom-call | flops 28000000000 | bytes 33554432 | tf_op jit(solution)/shard_map/exchange_1/pallas_call | solution.py:163
  226.8 0.1 all-gather.9.cloned.1.call-update
  226.9 0.1 all-gather.7.cloned.1.call-start
  227.0 0.7 all-gather.7.cloned.1.call-update
  227.7 128.1 %all-gather.11.cloned.1.call-done = bf16[2048,32,512]{2,1,0:T(8,128)(2,1)} async-done(((bf16[64,32,512]{2,1,0:T(8,128)(2,1)}), bf16[2048,32,512]{2,1,0:T(8,128)(2,1)}) %all-gather.11.cloned.1.call-update) | async-done | bytes 67108880 | tf_op jit(solution)/shard_map/all_gather | solution.py:243
  355.8 44.7 %place.3.refs_1_ = bf16[192,32,32,512]{3,2,1,0:T(8,128)(2,1)} custom-call(bf16[32,64,32,512]{3,2,1,0:T(8,128)(2,1)} %bitcast.2.refs_0_), custom_call_target="tpu_custom_call" | custom-call | flops 10000000 | bytes 134217728 | tf_op jit(solution)/shard_map/place/pallas_call | solution.py:203
  400.6 274.4 %all-gather.9.cloned.1.call-done = bf16[3456,32,512]{2,1,0:T(8,128)(2,1)} async-done(((bf16[108,32,512]{2,1,0:T(8,128)(2,1)}), bf16[3456,32,512]{2,1,0:T(8,128)(2,1)}) %all-gather.9.cloned.1.call-update) | async-done | bytes 113246224 | tf_op jit(solution)/shard_map/all_gather | solution.py:243
  675.0 76.7 %place.4.refs_1_ = bf16[192,32,32,512]{3,2,1,0:T(8,128)(2,1)} custom-call(bf16[32,108,32,512]{3,2,1,0:T(8,128)(2,1)} %bitcast.1.refs_0_, bf16[192,32,32,512]{3,2,1,0:T(8,128)(2,1)} %place.3.refs_1_), custom_call_target="tpu_custom_call", output_to_operand_aliasing={{}: (1, {})} | custom-call | flops 10000000 | bytes 226492416 | tf_op jit(solution)/shard_map/place/pallas_call | solution.py:203
  751.7 1.5 all-gather.7.cloned.1.call-done
  753.2 15.6 %place.5 = bf16[192,32,32,512]{3,2,1,0:T(8,128)(2,1)} custom-call(bf16[32,20,32,512]{3,2,1,0:T(8,128)(2,1)} %bitcast.4, bf16[192,32,32,512]{3,2,1,0:T(8,128)(2,1)} %place.4.refs_1_), custom_call_target="tpu_custom_call", output_to_operand_aliasing={{}: (1, {})} | custom-call | flops 10000000 | bytes 41943040 | tf_op jit(solution)/shard_map/place/pallas_call | solution.py:203
Async XLA Ops:
  7.2 348.6 %all-gather.11.cloned.1.call-start = ((), (), s32[]{:S(2)}) async-start(), calls=%async_computation.2 | async-start | bytes 69206016 | tf_op jit(solution)/shard_map/all_gather | solution.py:243
  78.1 596.9 %all-gather.9.cloned.1.call-start = ((), (), s32[]{:S(2)}) async-start(), calls=%async_computation.1 | async-start | bytes 116785152 | tf_op jit(solution)/shard_map/all_gather | solution.py:243
  226.9 526.3 %all-gather.7.cloned.1.call-start = ((), (), s32[]{:S(2)}) async-start(), calls=%async_computation | async-start | bytes 21626880 | tf_op jit(solution)/shard_map/all_gather | solution.py:243
Sparse Core Ops, SparseCore 0:
  78.3 277.5 all-gather.10
  357.9 317.0 all-gather.8
  677.1 76.0 all-gather.6

commit v3 on v2

--- a/solution.py
+++ b/solution.py
@@ -17,46 +17,22 @@
 COEF_C = 2.0315
 
 
-def momentum_kernel(*refs):
-    mom_ref, grad_ref = refs[:2]
-    new_ref, half_ref, sq_ref = refs[-3:]
-    mom_new = MOMENTUM * mom_ref[...] + grad_ref[...].astype(jnp.float32)
-    new_ref[...] = mom_new
-    half_ref[...] = mom_new.astype(jnp.bfloat16)
-    rows_sum = jnp.sum(mom_new * mom_new, axis=1)
-    lanes = sq_ref.shape[-1]
-    total = rows_sum[:, :lanes]
-    for start in range(lanes, rows_sum.shape[1], lanes):
-        total = total + rows_sum[:, start:start + lanes]
-    sq_ref[:, 0, 0] = total
-
-
-def momentum_step(mom_rows, grad_rows, mom_new, group, first, count):
+def momentum_kernel(mom_ref, grad_ref, new_ref):
+    new_ref[...] = MOMENTUM * mom_ref[...] + grad_ref[...].astype(jnp.float32)
+
+
+def momentum_step(mom_rows, grad_rows, steps):
     mats, rows, cols = mom_rows.shape
-    whole = pl.BlockSpec((group, rows, cols), lambda i: (first + i, 0, 0))
-    in_specs, operands, aliases = [whole, whole], [mom_rows, grad_rows], {}
-    if mom_new is not None:
-        in_specs.append(pl.BlockSpec(memory_space=pl.ANY))
-        operands.append(mom_new)
-        aliases = {2: 0}
+    spec = pl.BlockSpec((mats // steps, rows, cols), lambda i: (i, 0, 0))
     return pl.pallas_call(
         momentum_kernel,
-        grid=(count,),
-        out_shape=(
-            jax.ShapeDtypeStruct(mom_rows.shape, jnp.float32),
-            jax.ShapeDtypeStruct((count * group, rows, cols), jnp.bfloat16),
-            jax.ShapeDtypeStruct((group, count, 1, 128), jnp.float32),
-        ),
-        in_specs=in_specs,
-        out_specs=(
-            whole,
-            pl.BlockSpec((group, rows, cols), lambda i: (i, 0, 0)),
-            pl.BlockSpec((group, 1, 1, 128), lambda i: (0, i, 0, 0)),
-        ),
-        input_output_aliases=aliases,
-        cost_estimate=pl.CostEstimate(flops=10 * count * group * rows * cols, bytes_accessed=12 * count * group * rows * cols, transcendentals=0),
+        grid=(steps,),
+        out_shape=jax.ShapeDtypeStruct(mom_rows.shape, jnp.float32),
+        in_specs=[spec, spec],
+        out_specs=spec,
+        cost_estimate=pl.CostEstimate(flops=10 * mom_rows.size, bytes_accessed=10 * mom_rows.size, transcendentals=0),
         name="momentum_step",
-    )(*operands)
+    )(mom_rows, grad_rows)
 
 
 def remote(src, dst, send_sem, recv_sem, device):
@@ -80,16 +56,25 @@
     lax.fori_loop(1, group, send, 0)
 
 
-def exchange_kernel(group, first_mat, count, rms_scale, half_ref, sq_ref, w_ref, *refs):
-    outs = refs[:-11]
-    owned, ortho, x_buf, sq_buf, w_buf, in_sems, back_sems, sq_sems, own_sems, sq_own_sem, w_sem = refs[-11:]
+def exchange_kernel(group, first_mat, count, rms_scale, mom_ref, grad_ref, w_ref, *refs):
+    outs = refs[:-14]
+    (mom_buf, grad_buf, half_buf, sq_part, owned, ortho, x_buf, sq_buf, w_buf,
+     load_sems, in_sems, back_sems, sq_sems, w_sem) = refs[-14:]
     me = lax.axis_index("data")
     others = pl.ds(0, group - 1)
     rows, cols = owned.shape[-2:]
+    lanes = sq_buf.shape[-1]
+
+    def loads(chunk):
+        mats = pl.ds(first_mat + chunk * group, group)
+        return (pltpu.make_async_copy(mom_ref.at[mats], mom_buf.at[chunk], load_sems.at[chunk, 0]),
+                pltpu.make_async_copy(grad_ref.at[mats], grad_buf.at[chunk], load_sems.at[chunk, 1]))
+
+    for chunk in range(count):
+        for load in loads(chunk):
+            load.start()
     load_w = pltpu.make_async_copy(w_ref.at[pl.ds(first_mat, count * group)], w_buf, w_sem)
     load_w.start()
-    own_sq = pltpu.make_async_copy(sq_ref.at[me], sq_buf.at[me], sq_own_sem)
-    own_sq.start()
     barrier = pltpu.get_barrier_semaphore()
 
     def greet(step, carry):
@@ -97,26 +82,43 @@
         return carry
 
     lax.fori_loop(1, group, greet, 0)
+
+    def momentum(chunk):
+        for load in loads(chunk):
+            load.wait()
+
+        def one(mat, carry):
+            mom_new = MOMENTUM * mom_buf[chunk, mat] + grad_buf[chunk, mat].astype(jnp.float32)
+            half_buf[chunk, mat] = mom_new.astype(jnp.bfloat16)
+            rows_sum = jnp.sum(mom_new * mom_new, axis=0, keepdims=True)
+            total = rows_sum[:, :lanes]
+            for start in range(lanes, cols, lanes):
+                total = total + rows_sum[:, start:start + lanes]
+            sq_part[chunk, mat] = total
+            return carry
+
+        lax.fori_loop(0, group, one, 0, unroll=2)
+        owned[chunk, me] = half_buf[chunk, me]
+        sq_buf[chunk, me] = sq_part[chunk, me]
+
+    def send_in(chunk):
+        send_blocks(group, lambda i: sq_part.at[chunk, i], sq_buf, sq_sems, (chunk,))
+        send_blocks(group, lambda i: half_buf.at[chunk, i], owned, in_sems, (chunk,))
+
+    def later_chunk(chunk, carry):
+        momentum(chunk)
+        send_in(chunk)
+        return carry
+
+    momentum(0)
     pl.semaphore_wait(barrier, group - 1)
-
-    send_blocks(group, lambda i: sq_ref.at[i], sq_buf, sq_sems, ())
-
-    def own_block(chunk):
-        return pltpu.make_async_copy(half_ref.at[chunk * group + me], owned.at[chunk, me], own_sems.at[chunk])
-
-    def send_in(chunk, carry):
-        send_blocks(group, lambda i: half_ref.at[chunk * group + i], owned, in_sems, (chunk,))
-        own_block(chunk).start()
-        return carry
-
-    lax.fori_loop(0, count, send_in, 0)
-    own_sq.wait()
-    wait_bytes(sq_buf.at[others], sq_sems.at[1])
+    send_in(0)
+    lax.fori_loop(1, count, later_chunk, 0)
 
     def orthogonalize(chunk, carry):
-        own_block(chunk).wait()
+        wait_bytes(sq_buf.at[chunk, others], sq_sems.at[chunk, 1])
         wait_bytes(owned.at[chunk, others], in_sems.at[chunk, 1])
-        norm = jnp.sqrt(jnp.sum(sq_buf[:, chunk])) + NORM_EPS
+        norm = jnp.sqrt(jnp.sum(sq_buf[chunk])) + NORM_EPS
         x_mat = (owned[chunk].reshape(group * rows, cols).astype(jnp.float32) / norm).astype(jnp.bfloat16)
         for iteration in range(NS_ITERS):
             gram_mat = lax.dot_general(x_mat, x_mat, (((0,), (0,)), ((), ())), preferred_element_type=jnp.float32)
@@ -150,38 +152,43 @@
             if low_mat < high_mat:
                 lax.fori_loop(low_mat, high_mat, update, 0)
 
-    wait_bytes(sq_buf.at[others], sq_sems.at[0])
     for chunk in range(count):
+        wait_bytes(sq_buf.at[chunk, others], sq_sems.at[chunk, 0])
         wait_bytes(owned.at[chunk, others], in_sems.at[chunk, 0])
         wait_bytes(ortho.at[chunk, others], back_sems.at[chunk, 0])
 
 
-def exchange(group, half, sq_part, w_rows, first_mat, splits, rms_scale, collective_id):
-    mats, rows, cols = half.shape
-    count = mats // group
+def exchange(group, count, mom_rows, grad_rows, w_rows, first_mat, splits, rms_scale, collective_id):
+    rows, cols = mom_rows.shape[1:]
+    size = count * group * rows * cols
     block = pltpu.VMEM((count, group, rows, cols), jnp.bfloat16)
+    wide_block = pltpu.VMEM((count, group, rows, cols), jnp.float32)
+    sums = pltpu.VMEM((count, group, 1, 128), jnp.float32)
     return pl.pallas_call(
         functools.partial(exchange_kernel, group, first_mat, count, rms_scale),
         out_shape=[jax.ShapeDtypeStruct((split, rows, cols), jnp.bfloat16) for split in splits],
         in_specs=[pl.BlockSpec(memory_space=pl.ANY)] * 3,
         out_specs=[pl.BlockSpec(memory_space=pltpu.VMEM)] * len(splits),
         scratch_shapes=[
-            block,
-            block,
-            block,
-            pltpu.VMEM(sq_part.shape, jnp.float32),
-            pltpu.VMEM((mats, rows, cols), jnp.float32),
-            pltpu.SemaphoreType.DMA((count, 2)),
-            pltpu.SemaphoreType.DMA((count, 2)),
-            pltpu.SemaphoreType.DMA((2,)),
-            pltpu.SemaphoreType.DMA((count,)),
-            pltpu.SemaphoreType.DMA,
+            wide_block,
+            block,
+            block,
+            sums,
+            block,
+            block,
+            block,
+            sums,
+            pltpu.VMEM((count * group, rows, cols), jnp.float32),
+            pltpu.SemaphoreType.DMA((count, 2)),
+            pltpu.SemaphoreType.DMA((count, 2)),
+            pltpu.SemaphoreType.DMA((count, 2)),
+            pltpu.SemaphoreType.DMA((count, 2)),
             pltpu.SemaphoreType.DMA,
         ],
-        compiler_params=pltpu.CompilerParams(collective_id=collective_id, has_side_effects=True, vmem_limit_bytes=56 * 2**20),
-        cost_estimate=pl.CostEstimate(flops=count * 7 * 10**9, bytes_accessed=16 * half.size, transcendentals=0),
+        compiler_params=pltpu.CompilerParams(collective_id=collective_id, has_side_effects=True, vmem_limit_bytes=58 * 2**20),
+        cost_estimate=pl.CostEstimate(flops=count * 7 * 10**9, bytes_accessed=16 * size, transcendentals=0),
         name=f"exchange_{collective_id}",
-    )(half, sq_part, w_rows)
+    )(mom_rows, grad_rows, w_rows)
 
 
 def place_kernel(*refs):
@@ -232,16 +239,15 @@
         chunks = mat_count // group
         rms_scale = 0.2 * math.sqrt(max(rows_dev * group, col_count))
         shape = (mat_count, group, rows_dev, col_count)
-        mom_new, gathers, ahead = None, [], ()
+        gathers, ahead = [], ()
         for number, (first, count, splits) in enumerate(stage_plan(chunks, group)):
-            if mom_new is not None:
-                mom_new = after(mom_new, *ahead)
-            mom_new, half, sq_part = momentum_step(mom_rows, grad_rows, mom_new, group, first, count)
-            ahead = exchange(group, half, sq_part, w_rows, first * group, splits, rms_scale, number)
+            w_ahead = after(w_rows, *ahead)
+            ahead = exchange(group, count, mom_rows, grad_rows, w_ahead, first * group, splits, rms_scale, number)
             first_mat = first * group
             for w_new in ahead:
                 gathers.append((lax.all_gather(w_new, "data", axis=0, tiled=False), first_mat))
                 first_mat += w_new.shape[0]
+        mom_new = momentum_step(after(mom_rows, *ahead), grad_rows, chunks)
         params = None
         for gathered, first_mat in gathers:
             params = place(gathered, params, first_mat, shape, 4)

time: 776 us -> 768 us (0.990)
  waiting for transfers between devices: 405 us -> 390 us
    all_gather x3, waiting for transfers between devices: 404 us -> 390 us  [local_step(): lax.all_gather(w_new, 'data', axis=0, tiled=False)]
    pallas_call x2, Pallas kernels: 205 us -> 215 us  [exchange(): pl.pallas_call(functools.partial(exchange_kernel, group, first_mat, count...]
  transfers between devices with their start and end apart: 3 -> 3, of which waited for: 3 -> 3; matrix products, arithmetic and copies ran while one was open for 0% -> 0% of each run, Pallas kernels for 35% -> 36%
where the time goes in v3:
time: 768 us
  waiting for transfers between devices  390 us (51%)
  Pallas kernels  363 us (47%)
  between operations  13.8 us (2%)
    all_gather x3, waiting for transfers between devices, local_step(): lax.all_gather(w_new, 'data', axis=0, tiled=False)  390 us
    pallas_call x2, Pallas kernels, exchange(): pl.pallas_call(functools.partial(exchange_kernel, group, first_mat, count...  215 us
    pallas_call x3, Pallas kernels, place(): pl.pallas_call(place_kernel, grid=(steps,), out_shape=jax.ShapeDtypeStruc...  137 us
  transfers between devices with their start and end apart: 3, of which 3 were waited for; matrix products, arithmetic and copies ran while one was open for 0% of the time, Pallas kernels for 36%

profile of v3, /device:TPU:97, one launch (start us, length us, event | category | flops | bytes accessed | tf_op | source)
XLA Modules:
  0.0 767.6 jit_solution(6985201553922733658)
XLA Ops:
  7.2 0.1 all-gather.11.cloned.1.call-start
  7.2 67.9 %exchange_0.1 = bf16[64,32,512]{2,1,0:T(8,128)(2,1)} custom-call(f32[192,32,512]{2,1,0:T(8,128)} %mom_ref.4, bf16[192,32,512]{2,1,0:T(8,128)(2,1)} %grad_ref.5, f32[192,32,512]{2,1,0:T(8,128)} %w_ref.2), custom_call_target="tpu_custom_call" | custom-call | flops 14000000000 | bytes 16777216 | tf_op jit(solution)/shard_map/exchange_0/pallas_call | solution.py:167
  75.1 0.1 all-gather.11.cloned.1.call-update
  75.2 0.1 all-gather.9.cloned.1.call-start
  75.3 146.7 %exchange_1.1 = (bf16[108,32,512]{2,1,0:T(8,128)(2,1)}, bf16[20,32,512]{2,1,0:T(8,128)(2,1)}) custom-call(f32[192,32,512]{2,1,0:T(8,128)} %mom_ref.4, bf16[192,32,512]{2,1,0:T(8,128)(2,1)} %grad_ref.5, f32[192,32,512]{2,1,0:T(8,128)} %w_ref.2), custom_call_target="tpu_custom_call" | custom-call | flops 28000000000 | bytes 33554432 | tf_op jit(solution)/shard_map/exchange_1/pallas_call | solution.py:167
  222.0 0.1 all-gather.9.cloned.1.call-update
  222.0 0.1 all-gather.7.cloned.1.call-start
  222.1 0.7 all-gather.7.cloned.1.call-update
  222.8 11.7 %momentum_step.1 = f32[192,32,512]{2,1,0:T(8,128)} custom-call(f32[192,32,512]{2,1,0:T(8,128)} %mom_ref.4, bf16[192,32,512]{2,1,0:T(8,128)(2,1)} %grad_ref.5), custom_call_target="tpu_custom_call" | custom-call | flops 31457280 | bytes 31457280 | tf_op jit(solution)/shard_map/momentum_step/pallas_call | solution.py:27
  234.5 113.8 %all-gather.11.cloned.1.call-done = bf16[2048,32,512]{2,1,0:T(8,128)(2,1)} async-done(((bf16[64,32,512]{2,1,0:T(8,128)(2,1)}), bf16[2048,32,512]{2,1,0:T(8,128)(2,1)}) %all-gather.11.cloned.1.call-update) | async-done | bytes 67108880 | tf_op jit(solution)/shard_map/all_gather | solution.py:248
  348.2 44.7 %place.3.refs_1_ = bf16[192,32,32,512]{3,2,1,0:T(8,128)(2,1)} custom-call(bf16[32,64,32,512]{3,2,1,0:T(8,128)(2,1)} %bitcast.2.refs_0_), custom_call_target="tpu_custom_call" | custom-call | flops 10000000 | bytes 134217728 | tf_op jit(solution)/shard_map/place/pallas_call | solution.py:210
  393.0 274.2 %all-gather.9.cloned.1.call-done = bf16[3456,32,512]{2,1,0:T(8,128)(2,1)} async-done(((bf16[108,32,512]{2,1,0:T(8,128)(2,1)}), bf16[3456,32,512]{2,1,0:T(8,128)(2,1)}) %all-gather.9.cloned.1.call-update) | async-done | bytes 113246224 | tf_op jit(solution)/shard_map/all_gather | solution.py:248
  667.2 76.7 %place.4.refs_1_ = bf16[192,32,32,512]{3,2,1,0:T(8,128)(2,1)} custom-call(bf16[32,108,32,512]{3,2,1,0:T(8,128)(2,1)} %bitcast.1.refs_0_, bf16[192,32,32,512]{3,2,1,0:T(8,128)(2,1)} %place.3.refs_1_), custom_call_target="tpu_custom_call", output_to_operand_aliasing={{}: (1, {})} | custom-call | flops 10000000 | bytes 226492416 | tf_op jit(solution)/shard_map/place/pallas_call | solution.py:210
  743.9 1.5 all-gather.7.cloned.1.call-done
  745.4 15.6 %place.5 = bf16[192,32,32,512]{3,2,1,0:T(8,128)(2,1)} custom-call(bf16[32,20,32,512]{3,2,1,0:T(8,128)(2,1)} %bitcast.4, bf16[192,32,32,512]{3,2,1,0:T(8,128)(2,1)} %place.4.refs_1_), custom_call_target="tpu_custom_call", output_to_operand_aliasing={{}: (1, {})} | custom-call | flops 10000000 | bytes 41943040 | tf_op jit(solution)/shard_map/place/pallas_call | solution.py:210
Async XLA Ops:
  7.2 341.1 %all-gather.11.cloned.1.call-start = ((), (), s32[]{:S(2)}) async-start(), calls=%async_computation.2 | async-start | bytes 69206016 | tf_op jit(solution)/shard_map/all_gather | solution.py:248
  75.2 592.0 %all-gather.9.cloned.1.call-start = ((), (), s32[]{:S(2)}) async-start(), calls=%async_computation.1 | async-start | bytes 116785152 | tf_op jit(solution)/shard_map/all_gather | solution.py:248
  222.0 523.4 %all-gather.7.cloned.1.call-start = ((), (), s32[]{:S(2)}) async-start(), calls=%async_computation | async-start | bytes 21626880 | tf_op jit(solution)/shard_map/all_gather | solution.py:248
Sparse Core Ops, SparseCore 0:
  75.3 272.8 all-gather.10
  350.3 316.8 all-gather.8
  669.3 76.0 all-gather.6

commit v4 on v3

--- a/solution.py
+++ b/solution.py
@@ -47,9 +47,10 @@
 
 def send_blocks(group, source, landing, sems, lead):
     me = lax.axis_index("data")
+    stride = 7 if group % 7 else 1
 
     def send(step, carry):
-        target = lax.rem(me + step, group)
+        target = lax.rem(me + stride * step, group)
         remote(source(target), landing.at[(*lead, me)], sems.at[(*lead, 0)], sems.at[(*lead, 1)], target).start()
         return carry
 
@@ -97,7 +98,7 @@
             sq_part[chunk, mat] = total
             return carry
 
-        lax.fori_loop(0, group, one, 0, unroll=2)
+        lax.fori_loop(0, group, one, 0, unroll=4)
         owned[chunk, me] = half_buf[chunk, me]
         sq_buf[chunk, me] = sq_part[chunk, me]
 
@@ -150,7 +151,7 @@
                 return carry
 
             if low_mat < high_mat:
-                lax.fori_loop(low_mat, high_mat, update, 0)
+                lax.fori_loop(low_mat, high_mat, update, 0, unroll=4)
 
     for chunk in range(count):
         wait_bytes(sq_buf.at[chunk, others], sq_sems.at[chunk, 0])
@@ -191,16 +192,49 @@
     )(mom_rows, grad_rows, w_rows)
 
 
-def place_kernel(*refs):
-    gathered_ref, out_ref = refs[0], refs[-1]
-    for dev in range(gathered_ref.shape[0]):
-        out_ref[:, dev] = gathered_ref[dev]
-
-
-def place(gathered, params, first_mat, shape, block):
+def place_kernel(first_mat, block, lead, *refs):
+    gathered_ref, out_ref, buf, read_sems, write_sems = refs[0], *refs[-4:]
+    steps, slots = gathered_ref.shape[1] // block, buf.shape[0]
+
+    def read(step):
+        slot = lax.rem(step, slots)
+        return pltpu.make_async_copy(gathered_ref.at[:, pl.ds(step * block, block)], buf.at[slot], read_sems.at[slot])
+
+    def writes(step):
+        slot = lax.rem(step, slots)
+        mat = first_mat + step * block
+        return [pltpu.make_async_copy(buf.at[slot, :, i], out_ref.at[mat + i], write_sems.at[slot]) for i in range(block)]
+
+    def wait_writes(step):
+        slot = lax.rem(step, slots)
+        wait_bytes(buf.at[slot], write_sems.at[slot])
+
+    for step in range(min(lead, steps)):
+        read(step).start()
+
+    def one(step, carry):
+        read(step).wait()
+        for write in writes(step):
+            write.start()
+
+        @pl.when(step + lead < steps)
+        def _():
+            @pl.when(step + lead >= slots)
+            def _():
+                wait_writes(step + lead - slots)
+
+            read(step + lead).start()
+
+        return carry
+
+    lax.fori_loop(0, steps, one, 0)
+    for step in range(max(0, steps - slots), steps):
+        wait_writes(step)
+
+
+def place(gathered, params, first_mat, shape, block, slots):
     group, mats, rows, cols = gathered.shape
-    steps = mats // block
-    in_specs = [pl.BlockSpec((group, block, rows, cols), lambda i: (0, i, 0, 0))]
+    in_specs = [pl.BlockSpec(memory_space=pl.ANY)]
     operands = [gathered]
     aliases = {}
     if params is not None:
@@ -208,12 +242,17 @@
         operands.append(params)
         aliases = {1: 0}
     return pl.pallas_call(
-        place_kernel,
-        grid=(steps,),
+        functools.partial(place_kernel, first_mat, block, slots // 2),
         out_shape=jax.ShapeDtypeStruct(shape, gathered.dtype),
         in_specs=in_specs,
-        out_specs=pl.BlockSpec((block, group, rows, cols), lambda i: (first_mat // block + i, 0, 0, 0)),
+        out_specs=pl.BlockSpec(memory_space=pl.ANY),
+        scratch_shapes=[
+            pltpu.VMEM((slots, group, block, rows, cols), gathered.dtype),
+            pltpu.SemaphoreType.DMA((slots,)),
+            pltpu.SemaphoreType.DMA((slots,)),
+        ],
         input_output_aliases=aliases,
+        compiler_params=pltpu.CompilerParams(vmem_limit_bytes=40 * 2**20),
         cost_estimate=pl.CostEstimate(flops=1 * 10**7, bytes_accessed=4 * gathered.size, transcendentals=0),
         name="place",
     )(*operands)
@@ -250,7 +289,7 @@
         mom_new = momentum_step(after(mom_rows, *ahead), grad_rows, chunks)
         params = None
         for gathered, first_mat in gathers:
-            params = place(gathered, params, first_mat, shape, 4)
+            params = place(gathered, params, first_mat, shape, 2, 12)
         return params.reshape(mat_count, group * rows_dev, col_count), mom_new
 
     return jax.shard_map(local_step, mesh=mesh, in_specs=(row_spec, row_spec, row_spec), out_specs=(full_spec, row_spec), check_vma=False)

time: 768 us -> 762 us (level)
  Pallas kernels: 363 us -> 347 us
  waiting for transfers between devices: 390 us -> 400 us
    pallas_call x2, Pallas kernels: 215 us -> 203 us  [exchange(): pl.pallas_call(functools.partial(exchange_kernel, group, first_mat, count...]
    all_gather x3, waiting for transfers between devices: 390 us -> 399 us  [local_step(): lax.all_gather(w_new, 'data', axis=0, tiled=False)]
  transfers between devices with their start and end apart: 3 -> 3, of which waited for: 3 -> 3; matrix products, arithmetic and copies ran while one was open for 0% -> 0% of each run, Pallas kernels for 36% -> 35%
where the time goes in v4:
time: 762 us
  waiting for transfers between devices  400 us (52%)
  Pallas kernels  347 us (46%)
  between operations  13.8 us (2%)
    all_gather x3, waiting for transfers between devices, local_step(): lax.all_gather(w_new, 'data', axis=0, tiled=False)  399 us
    pallas_call x2, Pallas kernels, exchange(): pl.pallas_call(functools.partial(exchange_kernel, group, first_mat, count...  203 us
    pallas_call x3, Pallas kernels, place(): pl.pallas_call(functools.partial(place_kernel, first_mat, block, slots //...  133 us
  transfers between devices with their start and end apart: 3, of which 3 were waited for; matrix products, arithmetic and copies ran while one was open for 0% of the time, Pallas kernels for 35%

profile of v4, /device:TPU:97, one launch (start us, length us, event | category | flops | bytes accessed | tf_op | source)
XLA Modules:
  0.0 761.8 jit_solution(7731058194039901075)
XLA Ops:
  7.2 0.1 all-gather.11.cloned.1.call-start
  7.2 64.3 %exchange_0.1 = bf16[64,32,512]{2,1,0:T(8,128)(2,1)} custom-call(f32[192,32,512]{2,1,0:T(8,128)} %mom_ref.4, bf16[192,32,512]{2,1,0:T(8,128)(2,1)} %grad_ref.5, f32[192,32,512]{2,1,0:T(8,128)} %w_ref.2), custom_call_target="tpu_custom_call" | custom-call | flops 14000000000 | bytes 16777216 | tf_op jit(solution)/shard_map/exchange_0/pallas_call | solution.py:168
  71.6 0.1 all-gather.11.cloned.1.call-update
  71.6 0.1 all-gather.9.cloned.1.call-start
  71.7 138.4 %exchange_1.1 = (bf16[108,32,512]{2,1,0:T(8,128)(2,1)}, bf16[20,32,512]{2,1,0:T(8,128)(2,1)}) custom-call(f32[192,32,512]{2,1,0:T(8,128)} %mom_ref.4, bf16[192,32,512]{2,1,0:T(8,128)(2,1)} %grad_ref.5, f32[192,32,512]{2,1,0:T(8,128)} %w_ref.2), custom_call_target="tpu_custom_call" | custom-call | flops 28000000000 | bytes 33554432 | tf_op jit(solution)/shard_map/exchange_1/pallas_call | solution.py:168
  210.1 0.1 all-gather.9.cloned.1.call-update
  210.2 0.1 all-gather.7.cloned.1.call-start
  210.2 0.7 all-gather.7.cloned.1.call-update
  211.0 11.7 %momentum_step.1 = f32[192,32,512]{2,1,0:T(8,128)} custom-call(f32[192,32,512]{2,1,0:T(8,128)} %mom_ref.4, bf16[192,32,512]{2,1,0:T(8,128)(2,1)} %grad_ref.5), custom_call_target="tpu_custom_call" | custom-call | flops 31457280 | bytes 31457280 | tf_op jit(solution)/shard_map/momentum_step/pallas_call | solution.py:27
  222.6 122.7 %all-gather.11.cloned.1.call-done = bf16[2048,32,512]{2,1,0:T(8,128)(2,1)} async-done(((bf16[64,32,512]{2,1,0:T(8,128)(2,1)}), bf16[2048,32,512]{2,1,0:T(8,128)(2,1)}) %all-gather.11.cloned.1.call-update) | async-done | bytes 67108880 | tf_op jit(solution)/shard_map/all_gather | solution.py:287
  345.4 44.7 %place.3.refs_1_ = bf16[192,32,32,512]{3,2,1,0:T(8,128)(2,1)} custom-call(bf16[32,64,32,512]{3,2,1,0:T(8,128)(2,1)} %bitcast.2.refs_0_), custom_call_target="tpu_custom_call" | custom-call | flops 10000000 | bytes 134217728 | tf_op jit(solution)/shard_map/place/pallas_call | solution.py:244
  390.1 272.1 %all-gather.9.cloned.1.call-done = bf16[3456,32,512]{2,1,0:T(8,128)(2,1)} async-done(((bf16[108,32,512]{2,1,0:T(8,128)(2,1)}), bf16[3456,32,512]{2,1,0:T(8,128)(2,1)}) %all-gather.9.cloned.1.call-update) | async-done | bytes 113246224 | tf_op jit(solution)/shard_map/all_gather | solution.py:287
  662.2 73.6 %place.4.refs_1_ = bf16[192,32,32,512]{3,2,1,0:T(8,128)(2,1)} custom-call(bf16[32,108,32,512]{3,2,1,0:T(8,128)(2,1)} %bitcast.1.refs_0_, bf16[192,32,32,512]{3,2,1,0:T(8,128)(2,1)} %place.3.refs_1_), custom_call_target="tpu_custom_call", output_to_operand_aliasing={{}: (1, {})} | custom-call | flops 10000000 | bytes 226492416 | tf_op jit(solution)/shard_map/place/pallas_call | solution.py:244
  735.8 4.6 all-gather.7.cloned.1.call-done
  740.4 14.8 %place.5 = bf16[192,32,32,512]{3,2,1,0:T(8,128)(2,1)} custom-call(bf16[32,20,32,512]{3,2,1,0:T(8,128)(2,1)} %bitcast.4, bf16[192,32,32,512]{3,2,1,0:T(8,128)(2,1)} %place.4.refs_1_), custom_call_target="tpu_custom_call", output_to_operand_aliasing={{}: (1, {})} | custom-call | flops 10000000 | bytes 41943040 | tf_op jit(solution)/shard_map/place/pallas_call | solution.py:244
Async XLA Ops:
  7.2 338.2 %all-gather.11.cloned.1.call-start = ((), (), s32[]{:S(2)}) async-start(), calls=%async_computation.2 | async-start | bytes 69206016 | tf_op jit(solution)/shard_map/all_gather | solution.py:287
  71.6 590.6 %all-gather.9.cloned.1.call-start = ((), (), s32[]{:S(2)}) async-start(), calls=%async_computation.1 | async-start | bytes 116785152 | tf_op jit(solution)/shard_map/all_gather | solution.py:287
  210.2 530.3 %all-gather.7.cloned.1.call-start = ((), (), s32[]{:S(2)}) async-start(), calls=%async_computation | async-start | bytes 21626880 | tf_op jit(solution)/shard_map/all_gather | solution.py:287
Sparse Core Ops, SparseCore 0:
  71.8 273.5 all-gather.10
  347.4 314.7 all-gather.8
  664.3 76.0 all-gather.6
